TPU v7x, 256 devices: a whole 4x4x8 slice. The times are simulated.
256 devices in a mesh: seg: 16 (over y_hi, x, core), tok: 16 (over z, y_lo).
Axes of the slice: x: 4, y: 4 (y_hi: 2, y_lo: 2; y = y_hi * 2 + y_lo), z: 8, core: 2. Of those that a mesh axis runs over, the one named last changes fastest.
Arguments:
- value: bfloat16 [1048576, 128], P(('seg', 'tok')), may hold values from -6 to 6
- gate_in: bfloat16 [1048576, 128], P(('seg', 'tok')), may hold values from -6 to 6
- gate_out: bfloat16 [1048576, 128], P(('seg', 'tok')), may hold values from -6 to 6
- filter_spectrum: bfloat16 [2, 256, 512, 128], P(None, 'tok'), may hold values from -8 to 8, as said below
- skip_gain: float32 [128], replicated, may hold values from 0.25 to 2
Outputs:
- mixed_out: bfloat16 [1048576, 128], P(('seg', 'tok'))
Inputs may be any that keep to these rules, and one draw needn't show every extreme that they name: `filter_spectrum`: the response of a real filter whose taps beyond the first 65536 are zero, rounded.
All inputs are finite; a program needn't handle non-finite values.
Results may differ from a plain program's by a relative error of at most 0.0085.
Values may be sent and summed in bfloat16 or wider, within the bound.
No kernel may reach another device: no remote copies, remote signals or barrier semaphores. Data moves between devices by JAX's collectives and lax.ppermute only.
A program may use at most 128 MiB of HBM per device.

v0:
```python
import functools
import math

import jax
import jax.numpy as jnp
import numpy as np
from jax import lax
from jax.experimental import pallas as pl
from jax.experimental.pallas import tpu as pltpu
from jax.sharding import Mesh, PartitionSpec as P

N1 = 256
N2 = 512
HALF = N2 // 2
ROWS = N1 // 2
FFT = N1 * N2
LANES = 128
SEGS = 8
ROW_T = 8
WIDE = N2 + LANES

ALL = ("yh", "x", "core", "z", "yl")
GROUP = ("x", "core", "z", "yl")


def trig(rows, cols, modulus):
    product = (rows[:, None].astype(np.int64) * cols[None, :]) % modulus
    angle = product.astype(np.float64) * (2.0 * math.pi / modulus)
    return np.cos(angle), np.sin(angle)


def tables():
    rh, t, row = np.meshgrid(np.arange(2), np.arange(16), np.arange(8), indexing="ij")
    k1 = (16 * t + 8 * rh + row).reshape(-1)
    n1 = np.arange(N1)
    n2 = np.arange(N2)
    k2 = np.arange(HALF)
    cos_one, sin_one = trig(k1, n1, N1)
    first = np.concatenate([cos_one, -sin_one], axis=0)
    cos_two, sin_two = trig(n2, k2, N2)
    tw_cos, tw_sin = trig(k1, n2, FFT)
    last = np.concatenate([cos_one.T[:ROWS], -sin_one.T[:ROWS]], axis=1)
    half = lambda a: jnp.asarray(a, jnp.float32).astype(jnp.bfloat16)
    return (
        np.asarray(first, dtype=jnp.bfloat16),
        np.asarray(cos_two, dtype=jnp.bfloat16),
        np.asarray(sin_two, dtype=jnp.bfloat16),
        np.asarray(cos_two.T, dtype=jnp.bfloat16),
        np.asarray(sin_two.T, dtype=jnp.bfloat16),
        np.asarray(tw_cos, dtype=np.float32),
        np.asarray(tw_sin, dtype=np.float32),
        np.asarray(last, dtype=jnp.bfloat16),
    )


def conv_body(cur, prev, h_re, h_im, first, c2, s2, c3, s3, tc, ts, last, out):
    dot = functools.partial(jnp.dot, preferred_element_type=jnp.float32)
    data = jnp.concatenate([cur[...], prev[...]], axis=0)
    a = dot(first[...], data)
    a_re = a[:N1]
    a_im = a[N1:]
    tcv = tc[...]
    tsv = ts[...]
    b_re = a_re * tcv + a_im * tsv
    b_im = a_im * tcv - a_re * tsv
    parity = lax.broadcasted_iota(jnp.int32, (1, N2), 1) % 2
    sign = (1 - 2 * parity).astype(jnp.float32)
    nyq = jnp.sum(a_re[0:1] * sign, axis=1, keepdims=True)
    b_re = b_re.astype(jnp.bfloat16)
    b_im = b_im.astype(jnp.bfloat16)
    x_re = dot(b_re, c2[...]) + dot(b_im, s2[...])
    x_im = dot(b_im, c2[...]) - dot(b_re, s2[...])
    hr = h_re.astype(jnp.float32)
    hi = h_im.astype(jnp.float32)
    z_re = (x_re * hr - x_im * hi).astype(jnp.bfloat16)
    z_im = (x_re * hi + x_im * hr).astype(jnp.bfloat16)
    p_re = dot(z_re, c3[...]) - dot(z_im, s3[...])
    p_im = dot(z_im, c3[...]) + dot(z_re, s3[...])
    q_re = (p_re * tcv - p_im * tsv).astype(jnp.bfloat16)
    q_im = (p_im * tcv + p_re * tsv).astype(jnp.bfloat16)
    lastv = last[...]
    total = dot(lastv[:, :N1], q_re) + dot(lastv[:, N1:], q_im)
    total = total + (nyq * hi[0:1, 0:1]) * sign
    out[...] = (total * (2.0 / FFT)).astype(jnp.bfloat16)


def filter_parts(h):
    def part(p):
        rows = []
        for rh in range(2):
            rows.append(jnp.concatenate([h[p * 4 + rh * 2], h[p * 4 + rh * 2 + 1]], axis=1))
        return jnp.concatenate(rows, axis=0)

    return part(0), part(1)


def inner_kernel(cur, prev, h, *rest):
    h_re, h_im = filter_parts(h)
    conv_body(cur.at[0], prev.at[0], h_re, h_im, *rest[:-1], rest[-1].at[0])


def border_kernel(acc, cur, prev, h, *rest):
    h_re, h_im = filter_parts(h)
    conv_body(cur.at[0], prev.at[0], h_re, h_im, *rest[:-1], rest[-1].at[0])


def whole(a):
    return pl.BlockSpec(a.shape, lambda *_: (0,) * a.ndim)


FLOPS = 2 * (2 * N1 * N1 * N2 + 8 * N1 * N2 * HALF + ROWS * 2 * N1 * N2)


def convolve(recv, border, consts):
    hspec = pl.BlockSpec((SEGS, ROWS, LANES), lambda *_: (0, 0, N2 // LANES))
    params = pltpu.CompilerParams(vmem_limit_bytes=50 * 1024 * 1024)
    consts_spec = [whole(c) for c in consts]
    blk = (1, ROWS, N2)
    shape = jax.ShapeDtypeStruct((SEGS, ROWS, N2), jnp.bfloat16)
    inner = pl.pallas_call(
        inner_kernel,
        grid=(SEGS - 1,),
        in_specs=[
            pl.BlockSpec(blk, lambda i: (i + 1, 0, 0)),
            pl.BlockSpec(blk, lambda i: (i, 0, 0)),
            hspec,
        ]
        + consts_spec,
        out_specs=pl.BlockSpec(blk, lambda i: (i + 1, 0, 0)),
        out_shape=shape,
        compiler_params=params,
        cost_estimate=pl.CostEstimate(flops=7 * FLOPS, bytes_accessed=4 << 20, transcendentals=0),
        name="inner",
    )(recv, recv, recv, *consts)
    return pl.pallas_call(
        border_kernel,
        grid=(1,),
        in_specs=[
            pl.BlockSpec(memory_space=pl.ANY),
            pl.BlockSpec(blk, lambda i: (0, 0, 0)),
            pl.BlockSpec(blk, lambda i: (0, 0, 0)),
            hspec,
        ]
        + consts_spec,
        out_specs=pl.BlockSpec(blk, lambda i: (0, 0, 0)),
        out_shape=shape,
        input_output_aliases={0: 0},
        compiler_params=params,
        cost_estimate=pl.CostEstimate(flops=FLOPS, bytes_accessed=3 << 20, transcendentals=0),
        name="border",
    )(inner, recv, border, recv, *consts)


def shards(value, gate_in, gate_out, filter_spectrum, skip_gain):
    sl = lax.axis_index(("x", "core"))
    tok = lax.axis_index(("z", "yl"))
    channels = value.shape[1]
    gated = (value.astype(jnp.float32) * gate_in.astype(jnp.float32)).astype(jnp.bfloat16)
    part = sl // 4
    rh = (sl // 2) % 2
    kh = sl % 2
    piece = lax.dynamic_slice(
        filter_spectrum, (part, rh * ROW_T, kh * LANES, 0), (1, ROW_T, LANES, channels)
    )[0]
    edge = jnp.where(part == 0, piece[0, 0], filter_spectrum[0, 0, HALF])
    edge = edge * jnp.bfloat16(0.5)
    mine = (tok == 0) & (rh == 0) & (kh == 0)
    at_edge = (
        (lax.broadcasted_iota(jnp.int32, piece.shape, 0) == 0)
        & (lax.broadcasted_iota(jnp.int32, piece.shape, 1) == 0)
        & mine
    )
    piece = jnp.where(at_edge, edge[None, None, :], piece)
    send = jnp.concatenate([gated.reshape(ROW_T, N2, channels), piece], axis=1)
    send = jnp.transpose(send, (2, 0, 1))
    recv = lax.all_to_all(send, GROUP, split_axis=0, concat_axis=0, tiled=True)
    recv = recv.reshape(SEGS, ROWS, WIDE)
    border = lax.ppermute(recv[SEGS - 1 :, :, :N2], "yh", [(0, 1)])
    mixed = convolve(recv, border, tables())
    back = lax.all_to_all(
        mixed.reshape(SEGS * 16, ROW_T, N2), GROUP, split_axis=0, concat_axis=0, tiled=True
    )
    mixed = jnp.transpose(back, (1, 2, 0)).reshape(-1, channels)
    result = gate_out.astype(jnp.float32) * (
        mixed.astype(jnp.float32) + skip_gain[None, :] * gated.astype(jnp.float32)
    )
    return result.astype(jnp.bfloat16)


def solution(mesh):
    fine = Mesh(mesh.devices.reshape(2, 4, 2, 8, 2), ALL)
    return jax.shard_map(
        shards,
        mesh=fine,
        in_specs=(
            P(ALL, None),
            P(ALL, None),
            P(ALL, None),
            P(None, ("z", "yl"), None, None),
            P(),
        ),
        out_specs=P(ALL, None),
        check_vma=False,
    )
```

profile of v0, /device:TPU:1, one launch (start us, length us, event | category | flops | bytes accessed | tf_op | source)
XLA Modules:
  0.0 115.8 jit_solution(17629276776533971879)
XLA Ops:
  0.1 1.1 dynamic-slice_bitcast_fusion
  1.1 0.7 fusion.3
  1.8 1.1 and_select_fusion
  3.0 0.2 copy.16
  3.2 1.5 %multiply_convert_fusion = bf16[4096,128]{1,0:T(8,128)(2,1)S(1)} fusion(bf16[4096,128]{1,0:T(8,128)(2,1)S(1)} %copy-done.9, bf16[4096,128]{1,0:T(8,128)(2,1)} %param.13), kind=kLoop, calls=%fused_computation.4 | loop fusion | flops 2097152 | bytes 3145728 | tf_op jit(solution)/shard_map/convert_element_type | solution.py:158
  4.7 0.9 copy.15
  5.6 0.1 maximum_bitcast_fusion
  5.7 0.0 copy-start
  5.7 0.0 copy-start.1
  5.7 0.0 copy-start.2
  5.7 0.0 copy-start.3
  5.7 0.0 copy-start.4
  5.8 0.0 copy-start.5
  5.8 0.0 copy-start.6
  5.8 0.0 copy-start.7
  5.8 49.1 %all_to_all.10 = bf16[128,8,640]{2,1,0:T(8,128)(2,1)S(1)} all-to-all(bf16[128,8,640]{2,1,0:T(8,128)(2,1)S(1)} %maximum_bitcast_fusion), channel_id=1, replica_groups=mesh['yh'=2,'x'=4,'core'=2,'z'=8,'yl'=2] {'x','core','z','yl'}, dimensions={0} | all-to-all | bytes 2621440 | tf_op jit(solution)/shard_map/all_to_all | solution.py:176
  54.9 4.5 %collective-permute-start = (bf16[1,128,512]{2,1,0:T(8,128)(2,1)S(1)}, bf16[1,128,512]{2,1,0:T(8,128)(2,1)S(1)}, u32[]{:S(2)}, u32[]{:S(2)}) collective-permute-start(bf16[1,128,512]{2,1,0:T(8,128)(2,1)S(1)} %slice.13), channel_id=1, source_target_pairs={{0,128},{1,129},{2,130},{3,131},{4,132},{5,133},{6,134},{7,135},{8... | collective-permute-start | bytes 393224 | tf_op jit(solution)/shard_map/ppermute | solution.py:178
  59.6 11.2 %inner.1.acc = bf16[8,128,512]{2,1,0:T(8,128)(2,1)S(1)} custom-call(bf16[8,128,640]{2,1,0:T(8,128)(2,1)} %bitcast.23, bf16[8,128,640]{2,1,0:T(8,128)(2,1)} %bitcast.24, bf16[8,128,640]{2,1,0:T(8,128)(2,1)} %bitcast.25, bf16[512,256]{1,0:T(8,128)(2,1)S(1)} %copy-done.6, bf16[512,256]{1,0:T(8,128)(2,1)S(1)} %copy-done.5, bf16[512,256]{1,0:T(8,128)(2,1)S(1)} %copy-done.4, ...), custom_call_target="tpu_custom_call" | custom-call | flops 5167382528 | bytes 4194304 | tf_op jit(solution)/shard_map/inner/pallas_call | solution.py:120
  70.8 0.0 collective-permute-done.prev
  70.8 2.4 %border.1 = bf16[8,128,512]{2,1,0:T(8,128)(2,1)S(1)} custom-call(bf16[8,128,512]{2,1,0:T(8,128)(2,1)S(1)} %inner.1.acc, bf16[8,128,640]{2,1,0:T(8,128)(2,1)} %bitcast.26, bf16[1,128,512]{2,1,0:T(8,128)(2,1)S(1)} %collective-permute-done.prev, bf16[8,128,640]{2,1,0:T(8,128)(2,1)} %bitcast.27, ...), custom_call_target="tpu_custom_call", output_to_operand_aliasing={{}: (0, {})} | custom-call | flops 738197504 | bytes 3145728 | tf_op jit(solution)/shard_map/border/pallas_call | solution.py:135
  73.2 36.1 %all_to_all.11 = bf16[128,8,512]{2,1,0:T(8,128)(2,1)S(1)} all-to-all(bf16[128,8,512]{2,1,0:T(8,128)(2,1)S(1)} %bitcast.21), channel_id=1, replica_groups=mesh['yh'=2,'x'=4,'core'=2,'z'=8,'yl'=2] {'x','core','z','yl'}, dimensions={0} | all-to-all | bytes 2097152 | tf_op jit(solution)/shard_map/all_to_all | solution.py:180
  109.3 1.6 %convert_bitcast_fusion = f32[8,512,128]{1,0,2:T(8,128)} fusion(bf16[128,8,512]{2,1,0:T(8,128)(2,1)S(1)} %all_to_all.11), kind=kLoop, calls=%fused_computation.3 | loop fusion | flops 524288 | bytes 3145728 | tf_op jit(solution)/shard_map/convert_element_type | solution.py:185
  110.9 2.0 %copy.17 = f32[8,512,128]{2,1,0:T(8,128)S(1)} copy(f32[8,512,128]{1,0,2:T(8,128)} %convert_bitcast_fusion) | data formatting | bytes 4194304 | tf_op jit(solution)/shard_map/convert_element_type | solution.py:185
  112.9 2.9 %fusion.1 = bf16[4096,128]{1,0:T(8,128)(2,1)} fusion(f32[8,512,128]{2,1,0:T(8,128)S(1)} %copy.17, bf16[4096,128]{1,0:T(8,128)(2,1)S(1)} %multiply_convert_fusion, bf16[4096,128]{1,0:T(8,128)(2,1)} %param.15, f32[128]{0:T(128)S(1)} %copy-done.10), kind=kLoop, calls=%fused_computation.2 | loop fusion | flops 3145728 | bytes 5243392 | tf_op jit(solution)/shard_map/convert_element_type | solution.py:187
  (17 shorter events, 0.0 us)
Async XLA Ops:
  0.0 3.1 %copy-start.9 = (bf16[4096,128]{1,0:T(8,128)(2,1)S(1)}, bf16[4096,128]{1,0:T(8,128)(2,1)}, u32[]{:S(2)}) copy-start(bf16[4096,128]{1,0:T(8,128)(2,1)} %param.14) | copy-start | bytes 3145732
  5.7 53.8 %copy-start = (f32[256,512]{1,0:T(8,128)S(1)}, f32[256,512]{1,0:T(8,128)}, u32[]{:S(2)}) copy-start(f32[256,512]{1,0:T(8,128)} %constant.90.clone.rest_6_) | copy-start | bytes 1572868
  5.7 53.8 %copy-start.1 = (f32[256,512]{1,0:T(8,128)S(1)}, f32[256,512]{1,0:T(8,128)}, u32[]{:S(2)}) copy-start(f32[256,512]{1,0:T(8,128)} %constant.89.clone.rest_5_) | copy-start | bytes 1572868
  5.7 53.8 %copy-start.2 = (bf16[256,512]{1,0:T(8,128)(2,1)S(1)}, bf16[256,512]{1,0:T(8,128)(2,1)}, u32[]{:S(2)}) copy-start(bf16[256,512]{1,0:T(8,128)(2,1)} %constant.88.clone.rest_4_) | copy-start | bytes 786436
  5.7 53.8 %copy-start.3 = (bf16[256,512]{1,0:T(8,128)(2,1)S(1)}, bf16[256,512]{1,0:T(8,128)(2,1)}, u32[]{:S(2)}) copy-start(bf16[256,512]{1,0:T(8,128)(2,1)} %constant.87.clone.rest_3_) | copy-start | bytes 786436
  5.7 53.8 %copy-start.4 = (bf16[512,256]{1,0:T(8,128)(2,1)S(1)}, bf16[512,256]{1,0:T(8,128)(2,1)}, u32[]{:S(2)}) copy-start(bf16[512,256]{1,0:T(8,128)(2,1)} %constant.86.clone.rest_2_) | copy-start | bytes 786436
  5.8 53.8 %copy-start.5 = (bf16[512,256]{1,0:T(8,128)(2,1)S(1)}, bf16[512,256]{1,0:T(8,128)(2,1)}, u32[]{:S(2)}) copy-start(bf16[512,256]{1,0:T(8,128)(2,1)} %constant.85.clone.rest_1_) | copy-start | bytes 786436
  5.8 53.8 %copy-start.6 = (bf16[512,256]{1,0:T(8,128)(2,1)S(1)}, bf16[512,256]{1,0:T(8,128)(2,1)}, u32[]{:S(2)}) copy-start(bf16[512,256]{1,0:T(8,128)(2,1)} %constant.84.clone.rest_0_) | copy-start | bytes 786436
  5.8 53.8 %copy-start.7 = (bf16[128,512]{1,0:T(8,128)(2,1)S(1)}, bf16[128,512]{1,0:T(8,128)(2,1)}, u32[]{:S(2)}) copy-start(bf16[128,512]{1,0:T(8,128)(2,1)} %constant.91.clone.rest_7_) | copy-start | bytes 393220
  54.9 4.6 %copy-start.8 = (bf16[128,8,640]{2,1,0:T(8,128)(2,1)}, bf16[128,8,640]{2,1,0:T(8,128)(2,1)S(1)}, u32[]{:S(2)}) copy-start(bf16[128,8,640]{2,1,0:T(8,128)(2,1)S(1)} %all_to_all.10) | copy-start | bytes 3932164
  54.9 15.8 %collective-permute-start = (bf16[1,128,512]{2,1,0:T(8,128)(2,1)S(1)}, bf16[1,128,512]{2,1,0:T(8,128)(2,1)S(1)}, u32[]{:S(2)}, u32[]{:S(2)}) collective-permute-start(bf16[1,128,512]{2,1,0:T(8,128)(2,1)S(1)} %slice.13), channel_id=1, source_target_pairs={{0,128},{1,129},{2,130},{3,131},{4,132},{5,133},{6,134},{7,135},{8... | collective-permute-start | bytes 393224 | tf_op jit(solution)/shard_map/ppermute | solution.py:178
  110.9 2.0 %copy-start.10 = (f32[128]{0:T(128)S(1)}, f32[128]{0:T(128)}, u32[]{:S(2)}) copy-start(f32[128]{0:T(128)} %param.17) | copy-start | bytes 1540
where the time goes:
time: 116 us
  blocking collectives  85.2 us (73%)
  Pallas kernels  13.6 us (12%)
  other arithmetic  7.92 us (7%)
  starting transfers between devices  4.53 us (4%)
  local copies, waits for them, and re-layouts  4.22 us (4%)
    all_to_all x1, blocking collectives, shards(): recv = lax.all_to_all(send, GROUP, split_axis=0, concat_axis=0, tiled=True)  49.1 us
    all_to_all x1, blocking collectives, shards(): lax.all_to_all(mixed.reshape(SEGS * 16, ROW_T, N2), GROUP, split_axis=0,...  36.1 us
    pallas_call x1, Pallas kernels, convolve(): pl.pallas_call(inner_kernel, grid=(SEGS - 1,), in_specs=[pl.BlockSpec(blk...  11.2 us
    ppermute x1, starting transfers between devices, shards(): border = lax.ppermute(recv[SEGS - 1:, :, :N2], 'yh', [(0, 1)])  4.53 us
    convert_element_type x1, other arithmetic, shards(): return result.astype(jnp.bfloat16)  2.85 us
    pallas_call x1, Pallas kernels, convolve(): pl.pallas_call(border_kernel, grid=(1,), in_specs=[pl.BlockSpec(memory_sp...  2.43 us
  transfers between devices with their start and end apart: 1, of which 0 were waited for; matrix products, arithmetic and copies ran while one was open for 0% of the time, Pallas kernels for 10%

commit v1 on v0

v1 whole, which is shorter than its diff:
```python
import functools
import math

import jax
import jax.numpy as jnp
import numpy as np
from jax import lax
from jax.experimental import pallas as pl
from jax.experimental.pallas import tpu as pltpu
from jax.sharding import Mesh, PartitionSpec as P

N1 = 256
N2 = 512
HALF = N2 // 2
ROWS = N1 // 2
FFT = N1 * N2
LANES = 128
SEGS = 8
ROW_T = 8
WIDE = N2 + LANES

ALL = ("yh", "x", "core", "z", "yl")
GROUP = ("x", "core", "z", "yl")


def trig(rows, cols, modulus):
    product = (rows[:, None].astype(np.int64) * cols[None, :]) % modulus
    angle = product.astype(np.float64) * (2.0 * math.pi / modulus)
    return np.cos(angle), np.sin(angle)


def tables():
    rh, t, row = np.meshgrid(np.arange(2), np.arange(16), np.arange(8), indexing="ij")
    k1 = (16 * t + 8 * rh + row).reshape(-1)
    n1 = np.arange(N1)
    n2 = np.arange(N2)
    k2 = np.arange(HALF)
    cos_one, sin_one = trig(k1, n1, N1)
    first = np.concatenate([cos_one, -sin_one], axis=0)
    cos_two, sin_two = trig(n2, k2, N2)
    tw_cos, tw_sin = trig(k1, n2, FFT)
    last = np.concatenate([cos_one.T[:ROWS], -sin_one.T[:ROWS]], axis=1)
    half = lambda a: jnp.asarray(a, jnp.float32).astype(jnp.bfloat16)
    return (
        np.asarray(first, dtype=jnp.bfloat16),
        np.asarray(cos_two, dtype=jnp.bfloat16),
        np.asarray(sin_two, dtype=jnp.bfloat16),
        np.asarray(cos_two.T, dtype=jnp.bfloat16),
        np.asarray(sin_two.T, dtype=jnp.bfloat16),
        np.asarray(tw_cos, dtype=np.float32),
        np.asarray(tw_sin, dtype=np.float32),
        np.asarray(last, dtype=jnp.bfloat16),
    )


def dot(a, b):
    return jnp.dot(a, b, preferred_element_type=jnp.float32)


def one_segment(cur, prev, h_re, h_im, first, c2, s2, c3, s3, tc, ts, last):
    data = jnp.concatenate([cur, prev], axis=0)
    a = dot(first[...], data)
    a_re = a[:N1]
    a_im = a[N1:]
    b_re = (a_re * tc[...] + a_im * ts[...]).astype(jnp.bfloat16)
    b_im = (a_im * tc[...] - a_re * ts[...]).astype(jnp.bfloat16)
    parity = lax.broadcasted_iota(jnp.int32, (1, N2), 1) % 2
    sign = (1 - 2 * parity).astype(jnp.float32)
    nyq = jnp.sum(a_re[0:1] * sign, axis=1, keepdims=True)
    x_re = dot(b_re, c2[...]) + dot(b_im, s2[...])
    x_im = dot(b_im, c2[...]) - dot(b_re, s2[...])
    hr = h_re[...]
    hi = h_im[...]
    z_re = (x_re * hr - x_im * hi).astype(jnp.bfloat16)
    z_im = (x_re * hi + x_im * hr).astype(jnp.bfloat16)
    p_re = dot(z_re, c3[...]) - dot(z_im, s3[...])
    p_im = dot(z_im, c3[...]) + dot(z_re, s3[...])
    q_re = (p_re * tc[...] - p_im * ts[...]).astype(jnp.bfloat16)
    q_im = (p_im * tc[...] + p_re * ts[...]).astype(jnp.bfloat16)
    total = dot(last[:, :N1], q_re) + dot(last[:, N1:], q_im)
    total = total + (nyq * h_im[0:1, 0:1]) * sign
    return (total * (2.0 / FFT)).astype(jnp.bfloat16)


def filter_parts(recv, h_re, h_im):
    for p, ref in enumerate((h_re, h_im)):
        for rh in range(2):
            for kh in range(2):
                ref[rh * ROWS : (rh + 1) * ROWS, kh * LANES : (kh + 1) * LANES] = recv[
                    p * 4 + rh * 2 + kh, :, N2:
                ].astype(jnp.float32)


def inner_kernel(recv, first, c2, s2, c3, s3, tc, ts, last, out, h_re, h_im):
    filter_parts(recv, h_re, h_im)

    def step(s, carry):
        out[s] = one_segment(
            recv[s, :, :N2], recv[s - 1, :, :N2], h_re, h_im, first, c2, s2, c3, s3, tc, ts, last
        )
        return carry

    lax.fori_loop(1, SEGS, step, 0)


def border_kernel(acc, recv, border, first, c2, s2, c3, s3, tc, ts, last, out, h_re, h_im):
    filter_parts(recv, h_re, h_im)
    out[0] = one_segment(
        recv[0, :, :N2], border[...], h_re, h_im, first, c2, s2, c3, s3, tc, ts, last
    )


MACS = 2 * N1 * N1 * N2 + 8 * N1 * N2 * HALF + ROWS * 2 * N1 * N2
IN_VMEM = pl.BlockSpec(memory_space=pltpu.VMEM)


def convolve(recv, border, consts):
    params = pltpu.CompilerParams(vmem_limit_bytes=40 * 1024 * 1024)
    shape = jax.ShapeDtypeStruct((SEGS, ROWS, N2), jnp.bfloat16)
    scratch = [pltpu.VMEM((N1, HALF), jnp.float32)] * 2
    inner = pl.pallas_call(
        inner_kernel,
        in_specs=[IN_VMEM] * 9,
        out_specs=IN_VMEM,
        out_shape=shape,
        scratch_shapes=scratch,
        compiler_params=params,
        cost_estimate=pl.CostEstimate(flops=14 * MACS, bytes_accessed=4 << 20, transcendentals=0),
        name="inner",
    )(recv, *consts)
    return pl.pallas_call(
        border_kernel,
        in_specs=[IN_VMEM] * 11,
        out_specs=IN_VMEM,
        out_shape=shape,
        input_output_aliases={0: 0},
        scratch_shapes=scratch,
        compiler_params=params,
        cost_estimate=pl.CostEstimate(flops=2 * MACS, bytes_accessed=3 << 20, transcendentals=0),
        name="border",
    )(inner, recv, border, *consts)


def pack_kernel(sl, tok, value, gate_in, piece, nyquist, out, turned):
    j = pl.program_id(0)

    @pl.when(j < N2 // LANES)
    def _():
        for row in range(ROW_T):
            v = value[row].astype(jnp.float32) * gate_in[row].astype(jnp.float32)
            v = v.astype(jnp.bfloat16).astype(jnp.float32)
            turned[pl.ds(row, LANES, stride=ROW_T), :] = v.T

    @pl.when(j == N2 // LANES)
    def _():
        mine = (tok[0] == 0) & (sl[0] % 4 == 0)
        for row in range(ROW_T):
            v = piece[0, row].astype(jnp.float32)
            if row == 0:
                edge = jnp.where(sl[0] // 4 == 0, v[0:1], nyquist[0, 0, 0:1].astype(jnp.float32))
                at_edge = (lax.broadcasted_iota(jnp.int32, v.shape, 0) == 0) & mine
                v = jnp.where(at_edge, 0.5 * edge, v)
            turned[pl.ds(row, LANES, stride=ROW_T), :] = v.T

    out[...] = turned[...].reshape(LANES, ROW_T, LANES).astype(jnp.bfloat16)


def pack(sl, tok, value, gate_in, filter_spectrum):
    last = N2 // LANES - 1
    block = pl.BlockSpec((ROW_T, LANES, LANES), lambda j, sl, tok: (0, jnp.minimum(j, last), 0))
    return pl.pallas_call(
        pack_kernel,
        grid_spec=pltpu.PrefetchScalarGridSpec(
            num_scalar_prefetch=2,
            grid=(WIDE // LANES,),
            in_specs=[
                block,
                block,
                pl.BlockSpec(
                    (1, ROW_T, LANES, LANES),
                    lambda j, sl, tok: (sl[0] // 4, (sl[0] // 2) % 2, sl[0] % 2, 0),
                ),
                pl.BlockSpec((1, 1, 8, LANES), lambda j, sl, tok: (0, 0, HALF // 8, 0)),
            ],
            out_specs=pl.BlockSpec((LANES, ROW_T, LANES), lambda j, sl, tok: (0, 0, j)),
            scratch_shapes=[pltpu.VMEM((LANES * ROW_T, LANES), jnp.float32)],
        ),
        out_shape=jax.ShapeDtypeStruct((LANES, ROW_T, WIDE), jnp.bfloat16),
        cost_estimate=pl.CostEstimate(flops=1 << 20, bytes_accessed=3 << 20, transcendentals=0),
        name="pack",
    )(sl, tok, value, gate_in, filter_spectrum, filter_spectrum)


def finish_kernel(back, value, gate_in, gate_out, skip, out, turned):
    turned[...] = back[...].astype(jnp.float32).reshape(LANES * ROW_T, LANES)
    for row in range(ROW_T):
        mixed = turned[pl.ds(row, LANES, stride=ROW_T), :].T
        gated = value[row].astype(jnp.float32) * gate_in[row].astype(jnp.float32)
        gated = gated.astype(jnp.bfloat16).astype(jnp.float32)
        res = gate_out[row].astype(jnp.float32) * (mixed + skip[...] * gated)
        out[row] = res.astype(jnp.bfloat16)


def finish(back, value, gate_in, gate_out, skip):
    block = pl.BlockSpec((ROW_T, LANES, LANES), lambda j: (0, j, 0))
    return pl.pallas_call(
        finish_kernel,
        grid=(N2 // LANES,),
        in_specs=[
            pl.BlockSpec((LANES, ROW_T, LANES), lambda j: (0, 0, j)),
            block,
            block,
            block,
            pl.BlockSpec((1, LANES), lambda j: (0, 0)),
        ],
        out_specs=block,
        out_shape=jax.ShapeDtypeStruct((ROW_T, N2, LANES), jnp.bfloat16),
        scratch_shapes=[pltpu.VMEM((LANES * ROW_T, LANES), jnp.float32)],
        cost_estimate=pl.CostEstimate(flops=1 << 20, bytes_accessed=5 << 20, transcendentals=0),
        name="finish",
    )(back, value, gate_in, gate_out, skip)


def shards(value, gate_in, gate_out, filter_spectrum, skip_gain):
    sl = lax.axis_index(("x", "core")).reshape(1)
    tok = lax.axis_index(("z", "yl")).reshape(1)
    cut = lambda a: a.reshape(ROW_T, N2, LANES)
    value = cut(value)
    gate_in = cut(gate_in)
    gate_out = cut(gate_out)
    send = pack(sl, tok, value, gate_in, filter_spectrum)
    recv = lax.all_to_all(send, GROUP, split_axis=0, concat_axis=0, tiled=True)
    recv = recv.reshape(SEGS, ROWS, WIDE)
    border = lax.ppermute(recv[SEGS - 1, :, :N2], "yh", [(0, 1)])
    mixed = convolve(recv, border, tables())
    back = lax.all_to_all(
        mixed.reshape(SEGS * 16, ROW_T, N2), GROUP, split_axis=0, concat_axis=0, tiled=True
    )
    result = finish(back, value, gate_in, gate_out, skip_gain.reshape(1, LANES))
    return result.reshape(-1, LANES)


def solution(mesh):
    fine = Mesh(mesh.devices.reshape(2, 4, 2, 8, 2), ALL)
    return jax.shard_map(
        shards,
        mesh=fine,
        in_specs=(
            P(ALL, None),
            P(ALL, None),
            P(ALL, None),
            P(None, ("z", "yl"), None, None),
            P(),
        ),
        out_specs=P(ALL, None),
        check_vma=False,
    )
```

time: 116 us -> 111 us (0.957)
  other arithmetic: 7.92 us -> 0 us
  Pallas kernels: 13.6 us -> 19.9 us
  local copies, waits for them, and re-layouts: 4.22 us -> 0.05 us
    pallas_call x2 -> x4, Pallas kernels: 13.6 us -> 19.9 us  [the longest x1 9.77 us: convolve(): pl.pallas_call(inner_kernel, in_specs=[IN_VMEM] * 9, out_specs=IN_VMEM, o...]
    convert_element_type x3 -> x0, other arithmetic: 5.97 us -> none  [the longest x1 2.85 us: shards(): return result.astype(jnp.bfloat16)]
    convert_element_type x1 -> x0, local copies, waits for them, and re-layouts: 2 us -> none  [shards(): mixed.astype(jnp.float32) + skip_gain[None, :] * gated.astype(jnp.float32)]
  transfers between devices with their start and end apart: 1 -> 1, of which waited for: 0 -> 0; matrix products, arithmetic and copies ran while one was open for 0% -> 0% of each run, Pallas kernels for 10% -> 9%
where the time goes in v1:
time: 111 us; the launch traced here: 110 us
  blocking collectives  85.5 us (77%)
  Pallas kernels  19.9 us (18%)
  starting transfers between devices  4.53 us (4%)
    all_to_all x1, blocking collectives, shards(): recv = lax.all_to_all(send, GROUP, split_axis=0, concat_axis=0, tiled=True)  49.3 us
    all_to_all x1, blocking collectives, shards(): lax.all_to_all(mixed.reshape(SEGS * 16, ROW_T, N2), GROUP, split_axis=0,...  36.2 us
    pallas_call x1, Pallas kernels, convolve(): pl.pallas_call(inner_kernel, in_specs=[IN_VMEM] * 9, out_specs=IN_VMEM, o...  9.77 us
    ppermute x1, starting transfers between devices, shards(): border = lax.ppermute(recv[SEGS - 1, :, :N2], 'yh', [(0, 1)])  4.53 us
    pallas_call x1, Pallas kernels, pack(): pl.pallas_call(pack_kernel, grid_spec=pltpu.PrefetchScalarGridSpec(num_sc...  4.36 us
    pallas_call x1, Pallas kernels, finish(): pl.pallas_call(finish_kernel, grid=(N2 // LANES,), in_specs=[pl.BlockSpec...  4.35 us
  transfers between devices with their start and end apart: 1, of which 0 were waited for; matrix products, arithmetic and copies ran while one was open for 0% of the time, Pallas kernels for 9%

profile of v1, /device:TPU:1, one launch (start us, length us, event | category | flops | bytes accessed | tf_op | source)
XLA Modules:
  0.0 110.1 jit_solution(11957930810016052210)
XLA Ops:
  0.0 4.4 %pack.1 = bf16[128,8,640]{2,1,0:T(8,128)(2,1)} custom-call(s32[1]{0:T(128)} %bitcast.sl, s32[1]{0:T(128)} %bitcast.1.tok, bf16[8,512,128]{2,1,0:T(8,128)(2,1)} %bitcast.15, bf16[8,512,128]{2,1,0:T(8,128)(2,1)} %bitcast.17, bf16[2,16,512,128]{3,2,1,0:T(8,128)(2,1)} %nyquist.1, bf16[2,16,512,128]{3,2,1,0:T(8,128)(2,1)} %nyquist.1), custom_call_target="tpu_custom_call" | custom-call | flops 1048576 | bytes 3145728 | tf_op jit(solution)/shard_map/pack/pallas_call | solution.py:171
  4.4 0.0 copy-start
  4.4 0.0 copy-start.1
  4.4 0.0 copy-start.2
  4.4 0.0 copy-start.3
  4.4 0.0 copy-start.4
  4.4 0.0 copy-start.5
  4.4 0.0 copy-start.6
  4.4 0.0 copy-start.7
  4.4 49.3 %all_to_all.10 = bf16[128,8,640]{2,1,0:T(8,128)(2,1)S(1)} all-to-all(bf16[128,8,640]{2,1,0:T(8,128)(2,1)} %pack.1), channel_id=1, replica_groups=mesh['yh'=2,'x'=4,'core'=2,'z'=8,'yl'=2] {'x','core','z','yl'}, dimensions={0} | all-to-all | bytes 2621440 | tf_op jit(solution)/shard_map/all_to_all | solution.py:232
  53.8 4.5 %collective-permute-start = (bf16[128,512]{1,0:T(8,128)(2,1)S(1)}, bf16[128,512]{1,0:T(8,128)(2,1)S(1)}, u32[]{:S(2)}, u32[]{:S(2)}) collective-permute-start(bf16[128,512]{1,0:T(8,128)(2,1)S(1)} %slice_bitcast_fusion), channel_id=1, source_target_pairs={{0,128},{1,129},{2,130},{3,131},{4,132},{5,133},{6,134},{7,135},{8... | collective-permute-start | bytes 393224 | tf_op jit(solution)/shard_map/ppermute | solution.py:234
  58.3 0.0 copy-done
  58.3 0.0 copy-done.1
  58.3 0.0 copy-done.2
  58.4 0.0 copy-done.3
  58.4 0.0 copy-done.4
  58.4 0.0 copy-done.5
  58.4 0.0 copy-done.6
  58.4 0.0 copy-done.7
  58.4 9.8 %inner.1.acc = bf16[8,128,512]{2,1,0:T(8,128)(2,1)S(1)} custom-call(bf16[8,128,640]{2,1,0:T(8,128)(2,1)S(1)} %bitcast.12, bf16[512,256]{1,0:T(8,128)(2,1)S(1)} %copy-done.6, bf16[512,256]{1,0:T(8,128)(2,1)S(1)} %copy-done.5, bf16[512,256]{1,0:T(8,128)(2,1)S(1)} %copy-done.4, bf16[256,512]{1,0:T(8,128)(2,1)S(1)} %copy-done.3, bf16[256,512]{1,0:T(8,128)(2,1)S(1)} %copy-done.2, ...), custom_call_target="tpu_custom_call" | custom-call | flops 5167382528 | bytes 4194304 | tf_op jit(solution)/shard_map/inner/pallas_call | solution.py:121
  68.2 0.0 collective-permute-done.border
  68.2 1.4 %border.1 = bf16[8,128,512]{2,1,0:T(8,128)(2,1)S(1)} custom-call(bf16[8,128,512]{2,1,0:T(8,128)(2,1)S(1)} %inner.1.acc, bf16[8,128,640]{2,1,0:T(8,128)(2,1)S(1)} %bitcast.13, bf16[128,512]{1,0:T(8,128)(2,1)S(1)} %collective-permute-done.border, bf16[512,256]{1,0:T(8,128)(2,1)S(1)} %copy-done.6, ...), custom_call_target="tpu_custom_call", output_to_operand_aliasing={{}: (0, {})} | custom-call | flops 738197504 | bytes 3145728 | tf_op jit(solution)/shard_map/border/pallas_call | solution.py:131
  69.6 36.2 %all_to_all.11.back = bf16[128,8,512]{2,1,0:T(8,128)(2,1)} all-to-all(bf16[128,8,512]{2,1,0:T(8,128)(2,1)S(1)} %bitcast.14), channel_id=1, replica_groups=mesh['yh'=2,'x'=4,'core'=2,'z'=8,'yl'=2] {'x','core','z','yl'}, dimensions={0} | all-to-all | bytes 2097152 | tf_op jit(solution)/shard_map/all_to_all | solution.py:236
  105.8 4.4 %finish.1 = bf16[8,512,128]{2,1,0:T(8,128)(2,1)} custom-call(bf16[128,8,512]{2,1,0:T(8,128)(2,1)} %all_to_all.11.back, bf16[8,512,128]{2,1,0:T(8,128)(2,1)} %bitcast.16, bf16[8,512,128]{2,1,0:T(8,128)(2,1)} %bitcast.18, bf16[8,512,128]{2,1,0:T(8,128)(2,1)} %bitcast.19, f32[1,128]{1,0:T(1,128)} %bitcast.20), custom_call_target="tpu_custom_call" | custom-call | flops 1048576 | bytes 5242880 | tf_op jit(solution)/shard_map/finish/pallas_call | solution.py:206
  (1 shorter events, 0.0 us)
Async XLA Ops:
  4.4 54.0 %copy-start = (f32[256,512]{1,0:T(8,128)S(1)}, f32[256,512]{1,0:T(8,128)}, u32[]{:S(2)}) copy-start(f32[256,512]{1,0:T(8,128)} %constant.42.clone.ts) | copy-start | bytes 1572868
  4.4 54.0 %copy-start.1 = (f32[256,512]{1,0:T(8,128)S(1)}, f32[256,512]{1,0:T(8,128)}, u32[]{:S(2)}) copy-start(f32[256,512]{1,0:T(8,128)} %constant.41.clone.tc) | copy-start | bytes 1572868
  4.4 54.0 %copy-start.2 = (bf16[256,512]{1,0:T(8,128)(2,1)S(1)}, bf16[256,512]{1,0:T(8,128)(2,1)}, u32[]{:S(2)}) copy-start(bf16[256,512]{1,0:T(8,128)(2,1)} %constant.40.clone.s3) | copy-start | bytes 786436
  4.4 54.0 %copy-start.3 = (bf16[256,512]{1,0:T(8,128)(2,1)S(1)}, bf16[256,512]{1,0:T(8,128)(2,1)}, u32[]{:S(2)}) copy-start(bf16[256,512]{1,0:T(8,128)(2,1)} %constant.39.clone.c3) | copy-start | bytes 786436
  4.4 54.0 %copy-start.4 = (bf16[512,256]{1,0:T(8,128)(2,1)S(1)}, bf16[512,256]{1,0:T(8,128)(2,1)}, u32[]{:S(2)}) copy-start(bf16[512,256]{1,0:T(8,128)(2,1)} %constant.38.clone.s2) | copy-start | bytes 786436
  4.4 54.0 %copy-start.5 = (bf16[512,256]{1,0:T(8,128)(2,1)S(1)}, bf16[512,256]{1,0:T(8,128)(2,1)}, u32[]{:S(2)}) copy-start(bf16[512,256]{1,0:T(8,128)(2,1)} %constant.37.clone.c2) | copy-start | bytes 786436
  4.4 54.0 %copy-start.6 = (bf16[512,256]{1,0:T(8,128)(2,1)S(1)}, bf16[512,256]{1,0:T(8,128)(2,1)}, u32[]{:S(2)}) copy-start(bf16[512,256]{1,0:T(8,128)(2,1)} %constant.36.clone.first) | copy-start | bytes 786436
  4.4 54.0 %copy-start.7 = (bf16[128,512]{1,0:T(8,128)(2,1)S(1)}, bf16[128,512]{1,0:T(8,128)(2,1)}, u32[]{:S(2)}) copy-start(bf16[128,512]{1,0:T(8,128)(2,1)} %constant.43.clone.last) | copy-start | bytes 393220
  53.8 14.4 %collective-permute-start = (bf16[128,512]{1,0:T(8,128)(2,1)S(1)}, bf16[128,512]{1,0:T(8,128)(2,1)S(1)}, u32[]{:S(2)}, u32[]{:S(2)}) collective-permute-start(bf16[128,512]{1,0:T(8,128)(2,1)S(1)} %slice_bitcast_fusion), channel_id=1, source_target_pairs={{0,128},{1,129},{2,130},{3,131},{4,132},{5,133},{6,134},{7,135},{8... | collective-permute-start | bytes 393224 | tf_op jit(solution)/shard_map/ppermute | solution.py:234

commit v2 on v1

v2 whole, which is shorter than its diff:
```python
import functools
import math

import jax
import jax.numpy as jnp
import numpy as np
from jax import lax
from jax.experimental import pallas as pl
from jax.experimental.pallas import tpu as pltpu
from jax.sharding import Mesh, PartitionSpec as P

N1 = 256
N2 = 512
HALF = N2 // 2
ROWS = N1 // 2
FFT = N1 * N2
LANES = 128
SEGS = 8
ROW_T = 8
WIDE = N2 + LANES

ALL = ("yh", "x", "core", "z", "yl")
GROUP = ("x", "core", "z", "yl")


def trig(rows, cols, modulus):
    product = (rows[:, None].astype(np.int64) * cols[None, :]) % modulus
    angle = product.astype(np.float64) * (2.0 * math.pi / modulus)
    return np.cos(angle), np.sin(angle)


def tables():
    rh, t, row = np.meshgrid(np.arange(2), np.arange(16), np.arange(8), indexing="ij")
    k1 = (16 * t + 8 * rh + row).reshape(-1)
    n1 = np.arange(N1)
    n2 = np.arange(N2)
    k2 = np.arange(HALF)
    cos_one, sin_one = trig(k1, n1, N1)
    first = np.concatenate([cos_one, -sin_one], axis=0)
    cos_two, sin_two = trig(n2, k2, N2)
    tw_cos, tw_sin = trig(k1, n2, FFT)
    last = np.concatenate([cos_one.T[:ROWS], -sin_one.T[:ROWS]], axis=1)
    by_column = np.concatenate([first, cos_two, sin_two], axis=0)
    by_row = np.concatenate([cos_two.T, sin_two.T, last], axis=0)
    twiddles = np.concatenate([tw_cos, tw_sin], axis=0)
    return (
        np.asarray(by_column, dtype=jnp.bfloat16),
        np.asarray(by_row, dtype=jnp.bfloat16),
        np.asarray(twiddles, dtype=np.float32),
    )


def split_tables(by_column, by_row, twiddles):
    return (
        by_column.at[:N2],
        by_column.at[N2 : 2 * N2],
        by_column.at[2 * N2 :],
        by_row.at[:HALF],
        by_row.at[HALF:N2],
        twiddles.at[:N1],
        twiddles.at[N1:],
        by_row.at[N2:],
    )


def dot(a, b):
    return jnp.dot(a, b, preferred_element_type=jnp.float32)


def segments(pairs, outs, h_re, h_im, first, c2, s2, c3, s3, tc, ts, last):
    parity = lax.broadcasted_iota(jnp.int32, (1, N2), 1) % 2
    sign = (1 - 2 * parity).astype(jnp.float32)
    halves = []
    for cur, prev in pairs:
        a = dot(first[...], jnp.concatenate([cur, prev], axis=0))
        a_re = a[:N1]
        a_im = a[N1:]
        b_re = (a_re * tc[...] + a_im * ts[...]).astype(jnp.bfloat16)
        b_im = (a_im * tc[...] - a_re * ts[...]).astype(jnp.bfloat16)
        nyq = jnp.sum(a_re[0:1] * sign, axis=1, keepdims=True)
        halves.append((b_re, b_im, nyq))
    for (b_re, b_im, nyq), out in zip(halves, outs):
        x_re = dot(b_re, c2[...]) + dot(b_im, s2[...])
        x_im = dot(b_im, c2[...]) - dot(b_re, s2[...])
        hr = h_re[...]
        hi = h_im[...]
        z_re = (x_re * hr - x_im * hi).astype(jnp.bfloat16)
        z_im = (x_re * hi + x_im * hr).astype(jnp.bfloat16)
        p_re = dot(z_re, c3[...]) - dot(z_im, s3[...])
        p_im = dot(z_im, c3[...]) + dot(z_re, s3[...])
        q_re = (p_re * tc[...] - p_im * ts[...]).astype(jnp.bfloat16)
        q_im = (p_im * tc[...] + p_re * ts[...]).astype(jnp.bfloat16)
        total = dot(last[:, :N1], q_re) + dot(last[:, N1:], q_im)
        total = total + (nyq * h_im[0:1, 0:1]) * sign
        out[...] = (total * (2.0 / FFT)).astype(jnp.bfloat16)


def filter_parts(recv, h_re, h_im):
    for p, ref in enumerate((h_re, h_im)):
        for rh in range(2):
            for kh in range(2):
                ref[rh * ROWS : (rh + 1) * ROWS, kh * LANES : (kh + 1) * LANES] = recv[
                    p * 4 + rh * 2 + kh, :, N2:
                ].astype(jnp.float32)


def inner_kernel(recv, by_column, by_row, twiddles, out, h_re, h_im):
    filter_parts(recv, h_re, h_im)
    consts = (h_re, h_im) + split_tables(by_column, by_row, twiddles)

    def step(i, carry):
        s = 2 * i + 1
        segments(
            [(recv[s, :, :N2], recv[s - 1, :, :N2]), (recv[s + 1, :, :N2], recv[s, :, :N2])],
            [out.at[s], out.at[s + 1]],
            *consts,
        )
        return carry

    lax.fori_loop(0, (SEGS - 2) // 2, step, 0)


def border_kernel(yh, acc, recv, border, by_column, by_row, twiddles, out, h_re, h_im):
    filter_parts(recv, h_re, h_im)
    consts = (h_re, h_im) + split_tables(by_column, by_row, twiddles)
    before = jnp.where(yh[0] == 0, jnp.zeros_like(border), border[...])
    segments(
        [(recv[SEGS - 1, :, :N2], recv[SEGS - 2, :, :N2]), (recv[0, :, :N2], before)],
        [out.at[SEGS - 1], out.at[0]],
        *consts,
    )


MACS = 2 * N1 * N1 * N2 + 8 * N1 * N2 * HALF + ROWS * 2 * N1 * N2
IN_VMEM = pl.BlockSpec(memory_space=pltpu.VMEM)


def convolve(yh, recv, border, consts):
    params = pltpu.CompilerParams(vmem_limit_bytes=28 * 1024 * 1024)
    shape = jax.ShapeDtypeStruct((SEGS, ROWS, N2), jnp.bfloat16)
    scratch = [pltpu.VMEM((N1, HALF), jnp.float32)] * 2
    inner = pl.pallas_call(
        inner_kernel,
        in_specs=[IN_VMEM] * 4,
        out_specs=IN_VMEM,
        out_shape=shape,
        scratch_shapes=scratch,
        compiler_params=params,
        cost_estimate=pl.CostEstimate(flops=12 * MACS, bytes_accessed=4 << 20, transcendentals=0),
        name="inner",
    )(recv, *consts)
    return pl.pallas_call(
        border_kernel,
        in_specs=[pl.BlockSpec(memory_space=pltpu.SMEM)] + [IN_VMEM] * 6,
        out_specs=IN_VMEM,
        out_shape=shape,
        input_output_aliases={1: 0},
        scratch_shapes=scratch,
        compiler_params=params,
        cost_estimate=pl.CostEstimate(flops=4 * MACS, bytes_accessed=3 << 20, transcendentals=0),
        name="border",
    )(yh, inner, recv, border, *consts)


def edge_kernel(recv, out):
    out[...] = recv[SEGS - 1, :, :N2]


def edge(recv):
    return pl.pallas_call(
        edge_kernel,
        in_specs=[IN_VMEM],
        out_specs=IN_VMEM,
        out_shape=jax.ShapeDtypeStruct((ROWS, N2), jnp.bfloat16),
        compiler_params=pltpu.CompilerParams(vmem_limit_bytes=8 * 1024 * 1024),
        name="edge",
    )(recv)


CHUNKS = N2 // LANES
IN_SMEM = pl.BlockSpec(memory_space=pltpu.SMEM)
ANYWHERE = pl.BlockSpec(memory_space=pl.ANY)


def pack_kernel(sl, tok, value, gate_in, spectrum, out, vbuf, gbuf, pbuf, nbuf, turned, sems):
    part = sl[0] // 4
    rh = (sl[0] // 2) % 2
    kh = sl[0] % 2
    copies = []
    for j in range(CHUNKS):
        lanes = pl.ds(j * LANES, LANES)
        for i, (src, dst) in enumerate(((value, vbuf), (gate_in, gbuf))):
            copies.append(
                pltpu.make_async_copy(src.at[:, lanes, :], dst.at[:, lanes, :], sems.at[2 * j + i])
            )
    k_lanes = pl.ds(pl.multiple_of(kh * LANES, LANES), LANES)
    copies.append(
        pltpu.make_async_copy(
            spectrum.at[part, pl.ds(rh * ROW_T, ROW_T), k_lanes, :], pbuf, sems.at[2 * CHUNKS]
        )
    )
    copies.append(
        pltpu.make_async_copy(
            spectrum.at[0, 0, pl.ds(HALF, 8), :], nbuf, sems.at[2 * CHUNKS + 1]
        )
    )
    for copy in copies:
        copy.start()

    def place(j, row, v):
        turned[j % 2, pl.ds(row, LANES, stride=ROW_T), :] = v.T

    def write(j):
        lanes = slice(j * LANES, (j + 1) * LANES)
        out[:, :, lanes] = turned[j % 2].reshape(LANES, ROW_T, LANES).astype(jnp.bfloat16)

    for j in range(CHUNKS):
        copies[2 * j].wait()
        copies[2 * j + 1].wait()
        lanes = slice(j * LANES, (j + 1) * LANES)
        for row in range(ROW_T):
            v = vbuf[row, lanes].astype(jnp.float32) * gbuf[row, lanes].astype(jnp.float32)
            place(j, row, v.astype(jnp.bfloat16).astype(jnp.float32))
        write(j)
    copies[2 * CHUNKS].wait()
    copies[2 * CHUNKS + 1].wait()
    mine = (tok[0] == 0) & (sl[0] % 4 == 0)
    for row in range(ROW_T):
        v = pbuf[row].astype(jnp.float32)
        if row == 0:
            edge = jnp.where(part == 0, v[0:1], nbuf[0:1].astype(jnp.float32))
            at_edge = (lax.broadcasted_iota(jnp.int32, v.shape, 0) == 0) & mine
            v = jnp.where(at_edge, 0.5 * edge, v)
        place(CHUNKS, row, v)
    write(CHUNKS)


def pack(sl, tok, value, gate_in, filter_spectrum):
    return pl.pallas_call(
        pack_kernel,
        in_specs=[IN_SMEM, IN_SMEM, ANYWHERE, ANYWHERE, ANYWHERE],
        out_specs=IN_VMEM,
        out_shape=jax.ShapeDtypeStruct((LANES, ROW_T, WIDE), jnp.bfloat16),
        scratch_shapes=[
            pltpu.VMEM((ROW_T, N2, LANES), jnp.bfloat16),
            pltpu.VMEM((ROW_T, N2, LANES), jnp.bfloat16),
            pltpu.VMEM((ROW_T, LANES, LANES), jnp.bfloat16),
            pltpu.VMEM((8, LANES), jnp.bfloat16),
            pltpu.VMEM((2, LANES * ROW_T, LANES), jnp.float32),
            pltpu.SemaphoreType.DMA((2 * CHUNKS + 2,)),
        ],
        cost_estimate=pl.CostEstimate(flops=1 << 20, bytes_accessed=3 << 20, transcendentals=0),
        name="pack",
    )(sl, tok, value, gate_in, filter_spectrum)


def finish_kernel(back, value, gate_in, gate_out, skip, out, turned, obuf, sems):
    copies = []
    for j in range(CHUNKS):
        lanes = slice(j * LANES, (j + 1) * LANES)
        slot = j % 2
        turned[slot] = back[:, :, lanes].astype(jnp.float32).reshape(LANES * ROW_T, LANES)
        for row in range(ROW_T):
            mixed = turned[slot, pl.ds(row, LANES, stride=ROW_T), :].T
            gated = value[row, lanes].astype(jnp.float32) * gate_in[row, lanes].astype(jnp.float32)
            gated = gated.astype(jnp.bfloat16).astype(jnp.float32)
            res = gate_out[row, lanes].astype(jnp.float32) * (mixed + skip[...] * gated)
            obuf[row, lanes] = res.astype(jnp.bfloat16)
        where = pl.ds(j * LANES, LANES)
        copies.append(
            pltpu.make_async_copy(obuf.at[:, where, :], out.at[:, where, :], sems.at[j])
        )
        copies[-1].start()
    for copy in copies:
        copy.wait()


def finish(back, value, gate_in, gate_out, skip):
    return pl.pallas_call(
        finish_kernel,
        in_specs=[IN_VMEM] * 5,
        out_specs=ANYWHERE,
        out_shape=jax.ShapeDtypeStruct((ROW_T, N2, LANES), jnp.bfloat16),
        scratch_shapes=[
            pltpu.VMEM((2, LANES * ROW_T, LANES), jnp.float32),
            pltpu.VMEM((ROW_T, N2, LANES), jnp.bfloat16),
            pltpu.SemaphoreType.DMA((CHUNKS,)),
        ],
        compiler_params=pltpu.CompilerParams(vmem_limit_bytes=14 * 1024 * 1024),
        cost_estimate=pl.CostEstimate(flops=1 << 20, bytes_accessed=5 << 20, transcendentals=0),
        name="finish",
    )(back, value, gate_in, gate_out, skip)


def shards(value, gate_in, gate_out, filter_spectrum, skip_gain):
    sl = lax.axis_index(("x", "core")).reshape(1)
    tok = lax.axis_index(("z", "yl")).reshape(1)
    cut = lambda a: a.reshape(ROW_T, N2, LANES)
    value = cut(value)
    gate_in = cut(gate_in)
    gate_out = cut(gate_out)
    send = pack(sl, tok, value, gate_in, filter_spectrum)
    recv = lax.all_to_all(send, GROUP, split_axis=0, concat_axis=0, tiled=True)
    recv = recv.reshape(SEGS, ROWS, WIDE)
    border = lax.ppermute(edge(recv), "yh", [(0, 1), (1, 0)])
    mixed = convolve(lax.axis_index("yh").reshape(1), recv, border, tables())
    back = lax.all_to_all(
        mixed.reshape(SEGS * 16, ROW_T, N2), GROUP, split_axis=0, concat_axis=0, tiled=True
    )
    result = finish(back, value, gate_in, gate_out, skip_gain.reshape(1, LANES))
    return result.reshape(-1, LANES)


def solution(mesh):
    fine = Mesh(mesh.devices.reshape(2, 4, 2, 8, 2), ALL)
    return jax.shard_map(
        shards,
        mesh=fine,
        in_specs=(
            P(ALL, None),
            P(ALL, None),
            P(ALL, None),
            P(None, ("z", "yl"), None, None),
            P(),
        ),
        out_specs=P(ALL, None),
        check_vma=False,
    )
```

time: 111 us -> 104 us (0.937)
  blocking collectives: 85.5 us -> 36.2 us
  waiting for transfers between devices: 0.01 us -> 34.4 us
  starting transfers between devices: 4.53 us -> 17.6 us
  Pallas kernels: 19.9 us -> 14.3 us
    all_to_all x1 -> x0, blocking collectives: 49.3 us -> none  [shards(): recv = lax.all_to_all(send, GROUP, split_axis=0, concat_axis=0, tiled=True)]
    all_to_all x0 -> x1, waiting for transfers between devices: none -> 34.4 us  [shards(): recv = lax.all_to_all(send, GROUP, split_axis=0, concat_axis=0, tiled=True)]
    all_to_all x0 -> x1, starting transfers between devices: none -> 14.9 us  [shards(): recv = lax.all_to_all(send, GROUP, split_axis=0, concat_axis=0, tiled=True)]
    pallas_call x4 -> x5, Pallas kernels: 19.9 us -> 14.3 us  [the longest x1 7.16 us: convolve(): pl.pallas_call(inner_kernel, in_specs=[IN_VMEM] * 4, out_specs=IN_VMEM, o...]
    ppermute x1, starting transfers between devices: 4.53 us -> 2.71 us  [shards(): border = lax.ppermute(edge(recv), 'yh', [(0, 1), (1, 0)])]
  transfers between devices with their start and end apart: 1 -> 2, of which waited for: 0 -> 1; matrix products, arithmetic and copies ran while one was open for 0% -> 0% of each run, Pallas kernels for 9% -> 7%
where the time goes in v2:
time: 104 us
  blocking collectives  36.2 us (35%)
  waiting for transfers between devices  34.4 us (33%)
  starting transfers between devices  17.6 us (17%)
  Pallas kernels  14.3 us (14%)
  local copies, waits for them, and re-layouts  1.13 us (1%)
    all_to_all x1, blocking collectives, shards(): lax.all_to_all(mixed.reshape(SEGS * 16, ROW_T, N2), GROUP, split_axis=0,...  36.2 us
    all_to_all x1, waiting for transfers between devices, shards(): recv = lax.all_to_all(send, GROUP, split_axis=0, concat_axis=0, tiled=True)  34.4 us
    all_to_all x1, starting transfers between devices, shards(): recv = lax.all_to_all(send, GROUP, split_axis=0, concat_axis=0, tiled=True)  14.9 us
    pallas_call x1, Pallas kernels, convolve(): pl.pallas_call(inner_kernel, in_specs=[IN_VMEM] * 4, out_specs=IN_VMEM, o...  7.16 us
    pallas_call x1, Pallas kernels, pack(): pl.pallas_call(pack_kernel, in_specs=[IN_SMEM, IN_SMEM, ANYWHERE, ANYWHER...  3.15 us
    ppermute x1, starting transfers between devices, shards(): border = lax.ppermute(edge(recv), 'yh', [(0, 1), (1, 0)])  2.71 us
    pallas_call x1, Pallas kernels, convolve(): pl.pallas_call(border_kernel, in_specs=[pl.BlockSpec(memory_space=pltpu.S...  2.38 us
  transfers between devices with their start and end apart: 2, of which 1 were waited for; matrix products, arithmetic and copies ran while one was open for 0% of the time, Pallas kernels for 7%

profile of v2, /device:TPU:1, one launch (start us, length us, event | category | flops | bytes accessed | tf_op | source)
XLA Modules:
  0.0 103.8 jit_solution(5178380874340110879)
XLA Ops:
  0.0 3.1 %pack.1 = bf16[128,8,640]{2,1,0:T(8,128)(2,1)} custom-call(s32[1]{0:T(128)} %bitcast.1.sl, s32[1]{0:T(128)} %bitcast.2.tok, bf16[8,512,128]{2,1,0:T(8,128)(2,1)} %bitcast.14, bf16[8,512,128]{2,1,0:T(8,128)(2,1)} %bitcast.16, bf16[2,16,512,128]{3,2,1,0:T(8,128)(2,1)} %spectrum.1), custom_call_target="tpu_custom_call" | custom-call | flops 1048576 | bytes 3145728 | tf_op jit(solution)/shard_map/pack/pallas_call | solution.py:239
  3.2 0.0 copy-start.4
  3.2 14.9 %all-to-all-start = ((bf16[128,8,640]{2,1,0:T(8,128)(2,1)}), bf16[128,8,640]{2,1,0:T(8,128)(2,1)S(1)}, u32[]{:S(2)}, u32[]{:S(2)}) async-start(bf16[128,8,640]{2,1,0:T(8,128)(2,1)} %pack.1), calls=%async_computation | async-start | bytes 2621440 | tf_op jit(solution)/shard_map/all_to_all | solution.py:303
  18.1 0.0 copy-start.3
  18.1 34.4 %all-to-all-done = bf16[128,8,640]{2,1,0:T(8,128)(2,1)S(1)} async-done(((bf16[128,8,640]{2,1,0:T(8,128)(2,1)}), bf16[128,8,640]{2,1,0:T(8,128)(2,1)S(1)}, u32[]{:S(2)}, u32[]{:S(2)}) %all-to-all-start) | async-done | bytes 1310752 | tf_op jit(solution)/shard_map/all_to_all | solution.py:303
  52.5 2.7 %collective-permute-start = (bf16[128,512]{1,0:T(8,128)(2,1)S(1)}, bf16[128,512]{1,0:T(8,128)(2,1)S(1)}, u32[]{:S(2)}, u32[]{:S(2)}) collective-permute-start(bf16[128,512]{1,0:T(8,128)(2,1)S(1)} %edge.1), channel_id=1, source_target_pairs={{0,128},{128,0},{1,129},{129,1},{2,130},{130,2},{3,131},{131,3},{4... | collective-permute-start | bytes 393224 | tf_op jit(solution)/shard_map/ppermute | solution.py:305
  55.2 0.0 copy-done.4
  55.2 0.0 copy-done.3
  55.2 0.0 copy-start.5
  55.2 1.1 %copy-done.5 = bf16[640,512]{1,0:T(8,128)(2,1)S(1)} copy-done((bf16[640,512]{1,0:T(8,128)(2,1)S(1)}, bf16[640,512]{1,0:T(8,128)(2,1)}, u32[]{:S(2)}) %copy-start.5) | copy-done | bytes 655384
  56.3 7.2 %inner.1.acc = bf16[8,128,512]{2,1,0:T(8,128)(2,1)S(1)} custom-call(bf16[8,128,640]{2,1,0:T(8,128)(2,1)S(1)} %bitcast.11, bf16[1536,256]{1,0:T(8,128)(2,1)S(1)} %copy-done.4, bf16[640,512]{1,0:T(8,128)(2,1)S(1)} %copy-done.5, f32[512,512]{1,0:T(8,128)S(1)} %copy-done.3), custom_call_target="tpu_custom_call" | custom-call | flops 4429185024 | bytes 4194304 | tf_op jit(solution)/shard_map/inner/pallas_call | solution.py:142
  63.5 0.0 collective-permute-done.border
  63.5 0.0 copy-done.6
  63.5 0.0 copy-start.2
  63.5 2.4 %border.1 = bf16[8,128,512]{2,1,0:T(8,128)(2,1)S(1)} custom-call(s32[1]{0:T(128)} %bitcast.yh, bf16[8,128,512]{2,1,0:T(8,128)(2,1)S(1)} %inner.1.acc, bf16[8,128,640]{2,1,0:T(8,128)(2,1)S(1)} %bitcast.12, bf16[128,512]{1,0:T(8,128)(2,1)S(1)} %collective-permute-done.border, bf16[1536,256]{1,0:T(8,128)(2,1)S(1)} %copy-done.4, ...), custom_call_target="tpu_custom_call", output_to_operand_aliasing={{}: (1, {})} | custom-call | flops 1476395008 | bytes 3145728 | tf_op jit(solution)/shard_map/border/pallas_call | solution.py:152
  65.9 0.0 copy-start
  65.9 0.0 copy-start.1
  65.9 0.0 copy-start.7
  65.9 36.2 %all_to_all.10.back = bf16[128,8,512]{2,1,0:T(8,128)(2,1)S(1)} all-to-all(bf16[128,8,512]{2,1,0:T(8,128)(2,1)S(1)} %bitcast.13), channel_id=1, replica_groups=mesh['yh'=2,'x'=4,'core'=2,'z'=8,'yl'=2] {'x','core','z','yl'}, dimensions={0} | all-to-all | bytes 2097152 | tf_op jit(solution)/shard_map/all_to_all | solution.py:307
  102.2 0.0 copy-done.2
  102.2 0.0 copy-done
  102.2 0.0 copy-done.1
  102.2 0.0 copy-done.7
  102.2 1.6 %finish.1 = bf16[8,512,128]{2,1,0:T(8,128)(2,1)} custom-call(bf16[128,8,512]{2,1,0:T(8,128)(2,1)S(1)} %all_to_all.10.back, bf16[8,512,128]{2,1,0:T(8,128)(2,1)S(1)} %bitcast.15, bf16[8,512,128]{2,1,0:T(8,128)(2,1)S(1)} %bitcast.17, bf16[8,512,128]{2,1,0:T(8,128)(2,1)S(1)} %bitcast.18, f32[1,128]{1,0:T(1,128)S(1)} %bitcast.19), custom_call_target="tpu_custom_call" | custom-call | flops 1048576 | bytes 5242880 | tf_op jit(solution)/shard_map/finish/pallas_call | solution.py:279
  (2 shorter events, 0.0 us)
Async XLA Ops:
  3.2 52.1 %copy-start.4 = (bf16[1536,256]{1,0:T(8,128)(2,1)S(1)}, bf16[1536,256]{1,0:T(8,128)(2,1)}, u32[]{:S(2)}) copy-start(bf16[1536,256]{1,0:T(8,128)(2,1)} %constant.29.clone.by_column) | copy-start | bytes 2359300
  3.2 49.3 %all-to-all-start = ((bf16[128,8,640]{2,1,0:T(8,128)(2,1)}), bf16[128,8,640]{2,1,0:T(8,128)(2,1)S(1)}, u32[]{:S(2)}, u32[]{:S(2)}) async-start(bf16[128,8,640]{2,1,0:T(8,128)(2,1)} %pack.1), calls=%async_computation | async-start | bytes 2621440 | tf_op jit(solution)/shard_map/all_to_all | solution.py:303
  18.1 37.1 %copy-start.3 = (f32[512,512]{1,0:T(8,128)S(1)}, f32[512,512]{1,0:T(8,128)}, u32[]{:S(2)}) copy-start(f32[512,512]{1,0:T(8,128)} %constant.31.clone.twiddles) | copy-start | bytes 3145732
  52.5 11.0 %collective-permute-start = (bf16[128,512]{1,0:T(8,128)(2,1)S(1)}, bf16[128,512]{1,0:T(8,128)(2,1)S(1)}, u32[]{:S(2)}, u32[]{:S(2)}) collective-permute-start(bf16[128,512]{1,0:T(8,128)(2,1)S(1)} %edge.1), channel_id=1, source_target_pairs={{0,128},{128,0},{1,129},{129,1},{2,130},{130,2},{3,131},{131,3},{4... | collective-permute-start | bytes 393224 | tf_op jit(solution)/shard_map/ppermute | solution.py:305
  55.2 1.1 %copy-start.5 = (bf16[640,512]{1,0:T(8,128)(2,1)S(1)}, bf16[640,512]{1,0:T(8,128)(2,1)}, u32[]{:S(2)}) copy-start(bf16[640,512]{1,0:T(8,128)(2,1)} %constant.30.clone.by_row) | copy-start | bytes 1966084
  56.3 7.2 %copy-start.6 = (bf16[640,512]{1,0:T(8,128)(2,1)S(1)}, bf16[640,512]{1,0:T(8,128)(2,1)}, u32[]{:S(2)}) copy-start(bf16[640,512]{1,0:T(8,128)(2,1)} %constant.30.clone.by_row) | copy-start | bytes 1966084
  63.5 38.6 %copy-start.2 = (bf16[4096,128]{1,0:T(8,128)(2,1)S(1)}, bf16[4096,128]{1,0:T(8,128)(2,1)}, u32[]{:S(2)}) copy-start(bf16[4096,128]{1,0:T(8,128)(2,1)} %param.10) | copy-start | bytes 3145732
  65.9 36.3 %copy-start = (bf16[4096,128]{1,0:T(8,128)(2,1)S(1)}, bf16[4096,128]{1,0:T(8,128)(2,1)}, u32[]{:S(2)}) copy-start(bf16[4096,128]{1,0:T(8,128)(2,1)} %param.8) | copy-start | bytes 3145732
  65.9 36.2 %copy-start.1 = (bf16[4096,128]{1,0:T(8,128)(2,1)S(1)}, bf16[4096,128]{1,0:T(8,128)(2,1)}, u32[]{:S(2)}) copy-start(bf16[4096,128]{1,0:T(8,128)(2,1)} %param.9) | copy-start | bytes 3145732
  65.9 36.2 %copy-start.7 = (f32[128]{0:T(128)S(1)}, f32[128]{0:T(128)}, u32[]{:S(2)}) copy-start(f32[128]{0:T(128)} %param.12) | copy-start | bytes 1540
